TPU v7x, 512 devices: a whole 4x8x8 slice. The times are simulated.
512 devices in a mesh: zero: 64 (over z_hi, y, core), width: 8 (over z_lo, x).
Axes of the slice: x: 4, y: 8, z: 8 (z_hi: 4, z_lo: 2; z = z_hi * 2 + z_lo), core: 2. Of those that a mesh axis runs over, the one named last changes fastest.
Arguments:
- slopes_in: float32 [512, 128, 4096], P(None, 'zero', 'width'), may hold values from -6 to 6
- moments_in: float32 [512, 128, 4096], P(None, 'zero', 'width'), may hold values from -6 to 6
- weights_in: float32 [512, 128, 4096], P(None, 'zero', 'width'), may hold values from -0.1875 to 0.1875
Outputs:
- new_weights: float32 [512, 128, 4096], P(None, 'zero', 'width')
- new_momentum: float32 [512, 128, 4096], P(None, 'zero', 'width')
All inputs are finite; a program needn't handle non-finite values.
Results may differ from a plain program's by a relative error of at most 0.0001.
Values sent between devices are 32-bit elements; how exact they have to be, the bound alone decides.
A program may use at most 64 MiB of HBM per device.

v0:
```python
import jax
import jax.numpy as jnp
from jax import lax
from jax.sharding import PartitionSpec as P

ITERS = 3


hold_rate = 0.8
learn_rate = 0.8
decay_rate = 0.1


def body(slopes_in, moments_in, weights_in):
    new_momentum = hold_rate * moments_in + slopes_in
    direction = hold_rate * new_momentum + slopes_in
    moved = lax.all_to_all(direction, "zero", split_axis=0, concat_axis=1, tiled=True)
    whole = lax.all_to_all(moved, "width", split_axis=0, concat_axis=2, tiled=True)
    iterate = whole * lax.rsqrt(jnp.sum(whole * whole, axis=(1, 2), keepdims=True) + 1e-06)
    for step in range(ITERS):
        gram = jnp.einsum("mik,mjk->mij", iterate, iterate, precision=lax.Precision.HIGHEST)
        mixed = -4.775 * gram + 2.0315 * jnp.einsum(
            "mij,mjk->mik", gram, gram, precision=lax.Precision.HIGHEST
        )
        iterate = 3.4445 * iterate + jnp.einsum(
            "mij,mjk->mik", mixed, iterate, precision=lax.Precision.HIGHEST
        )
    iterate = lax.all_to_all(iterate, "width", split_axis=2, concat_axis=0, tiled=True)
    back = lax.all_to_all(iterate, "zero", split_axis=1, concat_axis=0, tiled=True)
    new_weights = (1.0 - learn_rate * decay_rate) * weights_in - learn_rate * back
    return (new_weights, new_momentum)


def solution(mesh):
    in_specs = (P(None, "zero", "width"), P(None, "zero", "width"), P(None, "zero", "width"))
    out_specs = (P(None, "zero", "width"), P(None, "zero", "width"))
    return jax.shard_map(body, mesh=mesh, in_specs=in_specs, out_specs=out_specs, check_vma=False)
```

profile of v0, /device:TPU:1, one launch (start us, length us, event | category | flops | bytes accessed | tf_op | source)
XLA Modules:
  0.0 242.2 jit_solution(3589901737893157943)
XLA Ops:
  0.6 4.7 %multiply_add_fusion = (f32[512,2,512]{2,1,0:T(2,128)S(1)}, f32[512,2,512]{2,1,0:T(2,128)}) fusion(f32[512,2,512]{2,1,0:T(2,128)} %param.3, f32[512,2,512]{2,1,0:T(2,128)} %param.4), kind=kLoop, calls=%fused_computation.11 | loop fusion | flops 2097152 | bytes 8388608 | tf_op jit(solution)/shard_map/add | solution.py:16
  5.3 70.1 %all_to_all.54 = f32[512,2,512]{2,1,0:T(2,128)S(1)} all-to-all(f32[512,2,512]{2,1,0:T(2,128)S(1)} %get-tuple-element.4), channel_id=1, replica_groups=mesh['zero'=64,'width'=8] {'zero'}, dimensions={0} | all-to-all | bytes 4194304 | tf_op jit(solution)/shard_map/all_to_all | solution.py:17
  75.4 0.8 copy.39
  76.2 2.4 %all_to_all.43 = f32[8,128,512]{2,1,0:T(8,128)} reshape(f32[8,64,2,512]{3,2,1,0:T(2,128)S(1)} %bitcast.52) | data formatting | bytes 4194304 | tf_op jit(solution)/shard_map/all_to_all | solution.py:17
  78.6 30.7 %all_to_all.55 = f32[8,128,512]{2,1,0:T(8,128)S(1)} all-to-all(f32[8,128,512]{2,1,0:T(8,128)} %all_to_all.43), channel_id=1, replica_groups=mesh['zero'=64,'width'=8] {'width'}, dimensions={0} | all-to-all | bytes 4194304 | tf_op jit(solution)/shard_map/all_to_all | solution.py:18
  109.4 1.1 multiply_reduce_fusion
  111.2 1.8 fusion.4
  113.2 2.7 %multiply_bitcast_fusion.1 = (f32[1,128,8,512]{3,1,2,0:T(8,128)}, f32[1,128,8,512]{3,1,2,0:T(8,128)}) fusion(f32[8,128,512]{2,1,0:T(8,128)S(1)} %all_to_all.55, f32[]{:T(128)S(6)} %rsqrt.4), kind=kLoop, calls=%fused_computation.14 | loop fusion | flops 1048576 | bytes 6291460 | tf_op jit(solution)/shard_map/mul | solution.py:19
  115.9 1.9 copy.27
  117.8 2.9 %copy.26 = f32[1,128,8,512]{1,3,2,0:T(8,128)} copy(f32[1,128,8,512]{3,1,2,0:T(8,128)} %get-tuple-element.7) | data formatting | bytes 4194304 | tf_op jit(solution)/shard_map/mul | solution.py:25
  120.7 3.0 %copy.28 = f32[128,4096]{1,0:T(8,128)} copy(f32[128,4096]{0,1:T(8,128)} %bitcast.53) | data formatting | bytes 4194304 | tf_op jit(solution)/shard_map/mul | solution.py:25
  123.7 3.6 %convolution_add_fusion.2 = f32[128,4096]{1,0:T(8,128)S(1)} fusion(f32[128,4096]{1,0:T(8,128)} %copy.28, f32[128,128]{1,0:T(8,128)S(1)} %fusion.9, f32[128,4096]{0,1:T(8,128)S(1)} %bitcast.49), kind=kOutput, calls=%fused_computation.3 | convolution fusion | flops 805830656 | bytes 6356992 | tf_op jit(solution)/shard_map/mij,mjk->mik/dot_general | solution.py:25
  127.3 1.8 fusion.11
  129.3 2.0 convolution_add_fusion.1
  131.3 1.8 fusion.12
  133.3 2.0 fusion
  135.4 3.7 %copy.29 = f32[1,128,4096]{1,0,2:T(1,128)} copy(f32[1,128,4096]{2,1,0:T(8,128)S(1)} %fusion) | data formatting | bytes 4194304 | tf_op jit(solution)/shard_map/add | solution.py:25
  139.1 27.8 %all_to_all.56 = f32[1,128,4096]{1,0,2:T(1,128)S(1)} all-to-all(f32[1,128,4096]{1,0,2:T(1,128)} %copy.29), channel_id=1, replica_groups=mesh['zero'=64,'width'=8] {'width'}, dimensions={2} | all-to-all | bytes 4194304 | tf_op jit(solution)/shard_map/all_to_all | solution.py:28
  166.9 2.0 copy.33
  168.8 68.3 %all_to_all.57 = f32[8,128,512]{2,0,1:T(8,128)S(1)} all-to-all(f32[8,128,512]{2,0,1:T(8,128)} %bitcast.55), channel_id=1, replica_groups=mesh['zero'=64,'width'=8] {'zero'}, dimensions={1} | all-to-all | bytes 4194304 | tf_op jit(solution)/shard_map/all_to_all | solution.py:29
  237.1 0.2 broadcast_multiply_fusion
  237.4 1.3 copy-done
  238.7 0.6 bitcast_subtract_fusion
  239.3 2.9 %copy.32 = f32[512,2,512]{2,1,0:T(2,128)} copy(f32[512,2,512]{2,0,1:T(8,128)S(1)} %bitcast_subtract_fusion) | data formatting | bytes 4194304
  (4 shorter events, 0.6 us)
Async XLA Ops:
  237.1 1.6 copy-start
where the time goes:
time: 245 us; the launch traced here: 242 us
  blocking collectives  197 us (80%)
  local copies, waits for them, and re-layouts  20.9 us (9%)
  matrix products  13.6 us (6%)
  other arithmetic  9.39 us (4%)
    all_to_all x1, blocking collectives, body(): lax.all_to_all(direction, 'zero', split_axis=0, concat_axis=1, tiled=True)  70.1 us
    all_to_all x1, blocking collectives, body(): lax.all_to_all(iterate, 'zero', split_axis=1, concat_axis=0, tiled=True)  68.3 us
    all_to_all x1, blocking collectives, body(): lax.all_to_all(moved, 'width', split_axis=0, concat_axis=2, tiled=True)  30.7 us
    all_to_all x1, blocking collectives, body(): lax.all_to_all(iterate, 'width', split_axis=2, concat_axis=0, tiled=True)  27.8 us
    dot_general x3, matrix products, body(): jnp.einsum('mij,mjk->mik', mixed, iterate, precision=lax.Precision.HIGHEST)  7.66 us
    mul x2, local copies, waits for them, and re-layouts, body(): 3.4445 * iterate  5.84 us
    dot_general x3, matrix products, body(): jnp.einsum('mik,mjk->mij', iterate, iterate, precision=lax.Precision.HIGH...  5.38 us

commit v1 on v0

v1 whole, which is shorter than its diff:
```python
import functools

import jax
import jax.numpy as jnp
from jax import lax
from jax.experimental import pallas as pl
from jax.experimental.pallas import tpu as pltpu
from jax.sharding import PartitionSpec as P

MESH = pl.DeviceIdType.MESH

hold_rate = 0.8
learn_rate = 0.8
decay_rate = 0.1

NX, NY, NZ, NC = 4, 8, 8, 2
NZC = NZ * NC
HALVES = 2
ROWS = 1024


def dot(a, b, contract):
    return lax.dot_general(
        a, b, (contract, ((), ())), precision=lax.Precision.HIGHEST, preferred_element_type=jnp.float32
    )


def place():
    zero = lax.axis_index("zero")
    width = lax.axis_index("width")
    core = lax.rem(zero, NC)
    y = lax.rem(zero // NC, NY)
    z = (zero // (NC * NY)) * 2 + width // NX
    x = lax.rem(width, NX)
    return x, y, z, core


def device(x, y, z, core):
    return (((z // 2) * NY + y) * NC + core, lax.rem(z, 2) * NX + x)


def ring_step(k, n):
    d = k // 2 + 1
    return d + lax.rem(k, 2) * (n - 2 * d)


def kernel(
    slopes, moments, weights, out, momentum,
    sl, mo, we, direct, t1, t2, r1, r2, xs, gs, gr, v1, v2, w1, w2, final,
    in_sem, y_send, y_recv, z_send, z_recv, x_send, x_recv,
):
    x, y, z, core = place()
    zc = z * NC + core

    def y_partner(k):
        return lax.rem(y + ring_step(k, NY), NY)

    def z_partner(k):
        pair = k // 2
        far = lax.rem(z + ring_step(pair, NZ), NZ)
        last = k // 14
        pz = far + last * (z - far)
        pc = lax.rem(core + lax.rem(k, 2) + last, NC)
        return pz, pc

    loads = []
    for u in range(2 * HALVES):
        rows = pl.ds(u * ROWS, ROWS)
        loads.append((
            pltpu.make_async_copy(slopes.at[rows], sl.at[rows], in_sem.at[u, 0]),
            pltpu.make_async_copy(moments.at[rows], mo.at[rows], in_sem.at[u, 1]),
        ))
    for a, b in loads:
        a.start()
        b.start()
    load_weights = pltpu.make_async_copy(weights, we, in_sem.at[2 * HALVES, 0])
    load_weights.start()

    barrier = pltpu.get_barrier_semaphore()

    def greet_y(k, carry):
        pl.semaphore_signal(barrier, inc=1, device_id=device(x, y_partner(k), z, core), device_id_type=MESH)
        return carry

    def greet_z(k, carry):
        pz, pc = z_partner(k)
        pl.semaphore_signal(barrier, inc=1, device_id=device(x, y, pz, pc), device_id_type=MESH)
        return carry

    def greet_x(k, carry):
        px = lax.rem(x + 1 + k, NX)
        pl.semaphore_signal(barrier, inc=1, device_id=device(px, y, z, core), device_id_type=MESH)
        return carry

    lax.fori_loop(0, NY - 1, greet_y, 0)
    lax.fori_loop(0, NZC - 1, greet_z, 0)
    lax.fori_loop(0, NX - 1, greet_x, 0)
    pl.semaphore_wait(barrier, (NY - 1) + (NZC - 1) + (NX - 1))

    def y_copy(s, k, src, dst):
        p = y_partner(k)
        return pltpu.make_async_remote_copy(
            src_ref=src(p), dst_ref=dst(y), send_sem=y_send.at[s, k], recv_sem=y_recv.at[s, k],
            device_id=device(x, p, z, core), device_id_type=MESH)

    def z_copy(s, k, src, dst):
        pz, pc = z_partner(k)
        return pltpu.make_async_remote_copy(
            src_ref=src(pz * NC + pc), dst_ref=dst(zc), send_sem=z_send.at[s, k], recv_sem=z_recv.at[s, k],
            device_id=device(x, y, pz, pc), device_id_type=MESH)

    def x_copy(h, k):
        px = lax.rem(x + 1 + k, NX)
        return pltpu.make_async_remote_copy(
            src_ref=gs.at[h], dst_ref=gr.at[h, x], send_sem=x_send.at[h, k], recv_sem=x_recv.at[h, k],
            device_id=device(px, y, z, core), device_id_type=MESH)

    def start(copy, steps, *args):
        def body(k, carry):
            copy(args[0], k, *args[1:]).start()
            return carry
        lax.fori_loop(0, steps, body, 0)

    def wait_recv(copy, steps, *args):
        def body(k, carry):
            copy(args[0], k, *args[1:]).wait_recv()
            return carry
        lax.fori_loop(0, steps, body, 0)

    def wait_send(copy, steps, *args):
        def body(k, carry):
            copy(args[0], k, *args[1:]).wait_send()
            return carry
        lax.fori_loop(0, steps, body, 0)

    def out1_a(h):
        return y_copy, NY - 1, 4 * h + 0, lambda p: direct.at[2 * h, pl.ds(p * 128, 128)], lambda p: t1.at[h, p]

    def out1_b(h):
        return z_copy, NZC - 1, 4 * h + 0, lambda p: direct.at[2 * h + 1, pl.ds(p * 64, 64)], lambda p: t2.at[h, p]

    def out2_a(h):
        return (z_copy, NZC - 1, 4 * h + 1, lambda p: t1.at[h, :, pl.ds(p * 8, 8)],
                lambda p: r1.at[h, p])

    def out2_b(h):
        return (y_copy, NY - 1, 4 * h + 1, lambda p: t2.at[h, :, pl.ds(p * 8, 8)],
                lambda p: r2.at[h, p])

    def back1_a(h):
        return z_copy, NZC - 1, 4 * h + 2, lambda p: v1.at[h, p], lambda p: w1.at[h, p]

    def back1_b(h):
        return y_copy, NY - 1, 4 * h + 2, lambda p: v2.at[h, p], lambda p: w2.at[h, p]

    def back2_a(h):
        return (y_copy, NY - 1, 4 * h + 3, lambda p: w1.at[h, :, p],
                lambda p: final.at[2 * h, pl.ds(p * 16, 16)])

    def back2_b(h):
        return (z_copy, NZC - 1, 4 * h + 3, lambda p: w2.at[h, :, p],
                lambda p: final.at[2 * h + 1, pl.ds(p * 8, 8)])

    for h in range(HALVES):
        for colour in range(2):
            u = 2 * h + colour
            loads[u][0].wait()
            loads[u][1].wait()
            rows = pl.ds(u * ROWS, ROWS)
            slope = sl[rows, :]
            fresh = hold_rate * mo[rows, :] + slope
            momentum[rows, :] = fresh
            direct[u] = hold_rate * fresh + slope
        start(*out1_a(h))
        start(*out1_b(h))
        t1[h, y] = direct[2 * h, pl.ds(pl.multiple_of(y * 128, 128), 128)]
        t2[h, zc] = direct[2 * h + 1, pl.ds(pl.multiple_of(zc * 64, 64), 64)]

    for h in range(HALVES):
        wait_recv(*out1_a(h))
        start(*out2_a(h))
        r1[h, zc] = t1[h, :, pl.ds(pl.multiple_of(zc * 8, 8), 8)]
        wait_recv(*out1_b(h))
        start(*out2_b(h))
        r2[h, y] = t2[h, :, pl.ds(pl.multiple_of(y * 8, 8), 8)]

    row_id = lax.broadcasted_iota(jnp.int32, (128, 128), 0)
    col_id = lax.broadcasted_iota(jnp.int32, (128, 128), 1)
    eye = (row_id == col_id).astype(jnp.float32)

    for h in range(HALVES):
        wait_recv(*out2_a(h))
        flat = r1.at[h].reshape(ROWS, 128)
        for zl in range(2):
            for ct in range(4):
                for row in range(2):
                    for zh in range(4):
                        xs[2 * h, pl.ds(row * 64 + zh * 16, 16), pl.ds((zl * 4 + ct) * 128, 128)] = flat[
                            pl.ds(zh * 256 + zl * 128 + ct * 2 + row, 16, stride=8), :]
        a = xs[2 * h]
        gs[h, 0] = dot(a, a, ((1,), (1,)))
        wait_recv(*out2_b(h))
        flat = r2.at[h].reshape(ROWS, 128)
        for zl in range(2):
            for ct in range(4):
                for row in range(2):
                    for zh in range(4):
                        for c in range(2):
                            xs[2 * h + 1, pl.ds(row * 64 + zh * 16 + c * 8, 8), pl.ds((zl * 4 + ct) * 128, 128)] = flat[
                                pl.ds(zh * 32 + zl * 16 + c * 8 + ct * 2 + row, 8, stride=128), :]
        a = xs[2 * h + 1]
        gs[h, 1] = dot(a, a, ((1,), (1,)))
        for k in range(NX - 1):
            x_copy(h, k).start()
        gr[h, x] = gs[h]
        for k in range(NX - 1):
            x_copy(h, k).wait_recv()
        for i in range(2):
            gram = (gr[h, 0, i] + gr[h, 1, i]) + (gr[h, 2, i] + gr[h, 3, i])
            scale = lax.rsqrt(jnp.sum(jnp.sum(gram * eye, axis=1, keepdims=True), axis=0, keepdims=True) + 1e-06)
            gram = gram * (scale * scale)
            total = scale * eye
            for step in range(3):
                mixed = 3.4445 * eye - 4.775 * gram + 2.0315 * dot(gram, gram, ((1,), (0,)))
                total = scale * mixed if step == 0 else dot(mixed, total, ((1,), (0,)))
                if step < 2:
                    gram = dot(dot(mixed, gram, ((1,), (0,))), mixed, ((1,), (0,)))
            new = dot(total, xs[2 * h + i], ((1,), (0,)))
            if i == 0:
                flat = v1.at[h].reshape(ROWS, 128)
                for zl in range(2):
                    for ct in range(4):
                        for row in range(2):
                            for zh in range(4):
                                flat[pl.ds(zh * 256 + zl * 128 + ct * 2 + row, 16, stride=8), :] = new[
                                    row * 64 + zh * 16:row * 64 + zh * 16 + 16, (zl * 4 + ct) * 128:(zl * 4 + ct + 1) * 128]
                start(*back1_a(h))
                w1[h, zc] = v1[h, zc]
            else:
                flat = v2.at[h].reshape(ROWS, 128)
                for zl in range(2):
                    for ct in range(4):
                        for row in range(2):
                            for zh in range(4):
                                for c in range(2):
                                    first = row * 64 + zh * 16 + c * 8
                                    flat[pl.ds(zh * 32 + zl * 16 + c * 8 + ct * 2 + row, 8, stride=128), :] = new[
                                        first:first + 8, (zl * 4 + ct) * 128:(zl * 4 + ct + 1) * 128]
                start(*back1_b(h))
                w2[h, y] = v2[h, y]

    for h in range(HALVES):
        wait_recv(*back1_b(h))
        start(*back2_b(h))
        final[2 * h + 1, pl.ds(zc * 8, 8)] = w2[h, :, zc]
        wait_recv(*back1_a(h))
        start(*back2_a(h))
        final[2 * h, pl.ds(y * 16, 16)] = w1[h, :, y]

    load_weights.wait()
    for h in range(HALVES):
        for colour, plan in ((0, back2_a), (1, back2_b)):
            wait_recv(*plan(h))
            u = 2 * h + colour
            rows = pl.ds(u * ROWS, ROWS)
            out[rows, :] = (1.0 - learn_rate * decay_rate) * we[rows, :] - learn_rate * final[u].reshape(ROWS, 128)

    for h in range(HALVES):
        for plan in (out1_a, out1_b, out2_a, out2_b, back1_a, back1_b, back2_a, back2_b):
            wait_send(*plan(h))
        for k in range(NX - 1):
            x_copy(h, k).wait_send()


def body(slopes_in, moments_in, weights_in):
    mats, side, wide = slopes_in.shape

    def flat(a):
        return a.reshape(mats, side, wide // 128, 128).transpose(0, 2, 1, 3).reshape(mats * side * wide // 128, 128)

    def whole(a):
        return a.reshape(mats, wide // 128, side, 128).transpose(0, 2, 1, 3).reshape(mats, side, wide)

    f32 = jnp.float32
    shape = (mats * side * wide // 128, 128)
    vmem = pltpu.VMEM
    dma = pltpu.SemaphoreType.DMA
    out, momentum = pl.pallas_call(
        kernel,
        out_shape=(jax.ShapeDtypeStruct(shape, f32),) * 2,
        in_specs=[pl.BlockSpec(memory_space=pltpu.HBM)] * 3,
        out_specs=[pl.BlockSpec(memory_space=pltpu.VMEM)] * 2,
        scratch_shapes=[
            vmem(shape, f32), vmem(shape, f32), vmem(shape, f32),
            vmem((4, ROWS, 128), f32),
            vmem((HALVES, NY, 128, 128), f32), vmem((HALVES, NZC, 64, 128), f32),
            vmem((HALVES, NZC, NY, 8, 128), f32), vmem((HALVES, NY, NZC, 8, 128), f32),
            vmem((2 * HALVES, 128, 1024), f32),
            vmem((HALVES, 2, 128, 128), f32), vmem((HALVES, NX, 2, 128, 128), f32),
            vmem((HALVES, NZC, NY, 8, 128), f32), vmem((HALVES, NY, NZC, 8, 128), f32),
            vmem((HALVES, NZC, NY, 8, 128), f32), vmem((HALVES, NY, NZC, 8, 128), f32),
            vmem((4, 128, 8, 128), f32),
            dma((2 * HALVES + 1, 2)),
            dma((4 * HALVES, NY - 1)), dma((4 * HALVES, NY - 1)),
            dma((4 * HALVES, NZC - 1)), dma((4 * HALVES, NZC - 1)),
            dma((HALVES, NX - 1)), dma((HALVES, NX - 1)),
        ],
        compiler_params=pltpu.CompilerParams(
            collective_id=0, has_side_effects=True, vmem_limit_bytes=48 * 1024 * 1024),
        name="exchange",
    )(flat(slopes_in), flat(moments_in), flat(weights_in))
    return whole(out), whole(momentum)


def solution(mesh):
    spec = P(None, "zero", "width")
    return jax.shard_map(body, mesh=mesh, in_specs=(spec,) * 3, out_specs=(spec,) * 2, check_vma=False)
```

time: 245 us -> 129 us (0.53)
  blocking collectives: 197 us -> 0 us
  Pallas kernels: 0 us -> 124 us
  local copies, waits for them, and re-layouts: 20.9 us -> 2.64 us
  matrix products: 13.6 us -> 0 us
  other arithmetic: 9.39 us -> 0 us
    all_to_all x4 -> x0, blocking collectives: 197 us -> none  [the longest x1 70.1 us: body(): lax.all_to_all(direction, 'zero', split_axis=0, concat_axis=1, tiled=True)]
    pallas_call x0 -> x1, Pallas kernels: none -> 124 us  [body(): pl.pallas_call(kernel, out_shape=(jax.ShapeDtypeStruct(shape, f32),) * 2,...]
    dot_general x9 -> x0, matrix products: 13.6 us -> none  [the longest x3 7.66 us: body(): jnp.einsum('mij,mjk->mik', mixed, iterate, precision=lax.Precision.HIGHEST)]
    mul x3 -> x0, local copies, waits for them, and re-layouts: 7.74 us -> none  [the longest x2 5.84 us: body(): 3.4445 * iterate]
    all_to_all x3 -> x0, local copies, waits for them, and re-layouts: 5.16 us -> none  [the longest x2 3.2 us: body(): lax.all_to_all(direction, 'zero', split_axis=0, concat_axis=1, tiled=True)]
    add x1 -> x0, other arithmetic: 4.69 us -> none  [body(): direction = hold_rate * new_momentum + slopes_in]
    add x1 -> x0, local copies, waits for them, and re-layouts: 3.7 us -> none  [body(): 3.4445 * iterate]
    mul x2 -> x0, other arithmetic: 2.98 us -> none  [the longest x1 2.73 us: body(): whole * lax.rsqrt(jnp.sum(whole * whole, axis=(1, 2), keepdims=True) + 1e...]
where the time goes in v1:
time: 129 us; the launch traced here: 127 us
  Pallas kernels  124 us (96%)
  local copies, waits for them, and re-layouts  2.64 us (2%)
    pallas_call x1, Pallas kernels, body(): pl.pallas_call(kernel, out_shape=(jax.ShapeDtypeStruct(shape, f32),) * 2,...  124 us
    unnamed x2, local copies, waits for them, and re-layouts  2.64 us

profile of v1, /device:TPU:1, one launch (start us, length us, event | category | flops | bytes accessed | tf_op | source)
XLA Modules:
  0.0 127.4 jit_solution(1226784785636006226)
XLA Ops:
  0.6 124.2 %exchange.1 = (f32[4096,128]{1,0:T(8,128)S(1)}, f32[4096,128]{1,0:T(8,128)S(1)}) custom-call(f32[4096,128]{1,0:T(8,128)} %bitcast.27, f32[4096,128]{1,0:T(8,128)} %bitcast.28, f32[4096,128]{1,0:T(8,128)} %bitcast.29), custom_call_target="tpu_custom_call" | custom-call | tf_op jit(solution)/shard_map/exchange/pallas_call | solution.py:288
  124.8 1.3 %copy.12 = f32[512,2,512]{2,1,0:T(2,128)} copy(f32[512,2,512]{2,1,0:T(2,128)S(1)} %bitcast.26) | data formatting | bytes 4194304
  126.1 1.3 %copy.13 = f32[512,2,512]{2,1,0:T(2,128)} copy(f32[512,2,512]{2,1,0:T(2,128)S(1)} %bitcast.25) | data formatting | bytes 4194304

commit v2 on v1

v2 whole, which is shorter than its diff:
```python
import functools

import jax
import jax.numpy as jnp
from jax import lax
from jax.experimental import pallas as pl
from jax.experimental.pallas import tpu as pltpu
from jax.sharding import PartitionSpec as P

MESH = pl.DeviceIdType.MESH

hold_rate = 0.8
learn_rate = 0.8
decay_rate = 0.1

NX, NY, NZ, NC = 4, 8, 8, 2
NZC = NZ * NC
HALVES = 2
ROWS = 1024


def dot(a, b, contract):
    return lax.dot_general(
        a, b, (contract, ((), ())), precision=lax.Precision.HIGHEST, preferred_element_type=jnp.float32
    )


def place():
    zero = lax.axis_index("zero")
    width = lax.axis_index("width")
    core = lax.rem(zero, NC)
    y = lax.rem(zero // NC, NY)
    z = (zero // (NC * NY)) * 2 + width // NX
    x = lax.rem(width, NX)
    return x, y, z, core


def device(x, y, z, core):
    return (((z // 2) * NY + y) * NC + core, lax.rem(z, 2) * NX + x)


def ring_step(k, n):
    d = (n - k) // 2
    return d + lax.rem(k, 2) * (n - 2 * d)


def kernel(
    slopes, moments, weights, out, momentum,
    sl, mo, we, direct, t1, t2, r1, r2, xs, gs, gr, v1, v2, w1, w2, final,
    in_sem, y_send, y_recv, z_send, z_recv, x_send, x_recv,
):
    x, y, z, core = place()
    zc = z * NC + core

    def y_partner(k):
        return lax.rem(y + ring_step(k, NY), NY)

    def z_partner(k):
        pair = k // 2
        far = lax.rem(z + ring_step(pair, NZ), NZ)
        last = k // 14
        pz = far + last * (z - far)
        pc = lax.rem(core + lax.rem(k, 2) + last, NC)
        return pz, pc

    barrier = pltpu.get_barrier_semaphore()

    def greet_y(k, carry):
        pl.semaphore_signal(barrier, inc=1, device_id=device(x, y_partner(k), z, core), device_id_type=MESH)
        return carry

    def greet_z(k, carry):
        pz, pc = z_partner(k)
        pl.semaphore_signal(barrier, inc=1, device_id=device(x, y, pz, pc), device_id_type=MESH)
        return carry

    def greet_x(k, carry):
        px = lax.rem(x + 1 + k, NX)
        pl.semaphore_signal(barrier, inc=1, device_id=device(px, y, z, core), device_id_type=MESH)
        return carry

    lax.fori_loop(0, NZC - 1, greet_z, 0)
    lax.fori_loop(0, NY - 1, greet_y, 0)
    lax.fori_loop(0, NX - 1, greet_x, 0)
    loads = []
    for u in range(2 * HALVES):
        rows = pl.ds(u * ROWS, ROWS)
        loads.append((
            pltpu.make_async_copy(slopes.at[rows], sl.at[rows], in_sem.at[u, 0]),
            pltpu.make_async_copy(moments.at[rows], mo.at[rows], in_sem.at[u, 1]),
        ))
    for a, b in loads:
        a.start()
        b.start()
    load_weights = pltpu.make_async_copy(weights, we, in_sem.at[2 * HALVES, 0])
    load_weights.start()


    def y_copy(s, k, src, dst):
        p = y_partner(k)
        return pltpu.make_async_remote_copy(
            src_ref=src(p), dst_ref=dst(y), send_sem=y_send.at[s], recv_sem=y_recv.at[s],
            device_id=device(x, p, z, core), device_id_type=MESH)

    def z_copy(s, k, src, dst):
        pz, pc = z_partner(k)
        return pltpu.make_async_remote_copy(
            src_ref=src(pz * NC + pc), dst_ref=dst(zc), send_sem=z_send.at[s], recv_sem=z_recv.at[s],
            device_id=device(x, y, pz, pc), device_id_type=MESH)

    def x_copy(s, px):
        return pltpu.make_async_remote_copy(
            src_ref=gs.at[s], dst_ref=gr.at[s, x], send_sem=x_send.at[s], recv_sem=x_recv.at[s],
            device_id=device(px, y, z, core), device_id_type=MESH)

    def x_all(s):
        whole = gr.at[s, pl.ds(0, NX - 1)]
        return pltpu.make_async_remote_copy(
            src_ref=whole, dst_ref=whole, send_sem=x_send.at[s], recv_sem=x_recv.at[s],
            device_id=device(lax.rem(x + 1, NX), y, z, core), device_id_type=MESH)

    def start(copy, steps, slot, src, dst, whole):
        def body(k, carry):
            copy(slot, k, src, dst).start()
            return carry
        lax.fori_loop(0, steps, body, 0)

    def wait_recv(copy, steps, slot, src, dst, whole):
        copy(slot, 0, lambda p: whole, lambda p: whole).wait_recv()

    def wait_send(copy, steps, slot, src, dst, whole):
        copy(slot, 0, lambda p: whole, lambda p: whole).wait_send()

    def out1_a(h):
        return (y_copy, NY - 1, 4 * h, lambda p: direct.at[2 * h, pl.ds(p * 128, 128)], lambda p: t1.at[h, p],
                t1.at[h, pl.ds(0, NY - 1)])

    def out1_b(h):
        return (z_copy, NZC - 1, 4 * h, lambda p: direct.at[2 * h + 1, pl.ds(p * 64, 64)], lambda p: t2.at[h, p],
                t2.at[h, pl.ds(0, NZC - 1)])

    def out2_a(h):
        return (z_copy, NZC - 1, 4 * h + 1, lambda p: t1.at[h, :, pl.ds(p * 8, 8)], lambda p: r1.at[h, p],
                r1.at[h, pl.ds(0, NZC - 1)])

    def out2_b(h):
        return (y_copy, NY - 1, 4 * h + 1, lambda p: t2.at[h, :, pl.ds(p * 8, 8)], lambda p: r2.at[h, p],
                r2.at[h, pl.ds(0, NY - 1)])

    def back1_a(h):
        return (z_copy, NZC - 1, 4 * h + 2, lambda p: v1.at[h, p], lambda p: w1.at[h, p],
                w1.at[h, pl.ds(0, NZC - 1)])

    def back1_b(h):
        return (y_copy, NY - 1, 4 * h + 2, lambda p: v2.at[h, p], lambda p: w2.at[h, p],
                w2.at[h, pl.ds(0, NY - 1)])

    def back2_a(h):
        return (y_copy, NY - 1, 4 * h + 3, lambda p: w1.at[h, :, p], lambda p: final.at[2 * h, pl.ds(p * 16, 16)],
                final.at[2 * h, pl.ds(0, 16 * (NY - 1))])

    def back2_b(h):
        return (z_copy, NZC - 1, 4 * h + 3, lambda p: w2.at[h, :, p], lambda p: final.at[2 * h + 1, pl.ds(p * 8, 8)],
                final.at[2 * h + 1, pl.ds(0, 8 * (NZC - 1))])

    def take(h, i):
        flat = (r1, r2)[i].at[h].reshape(ROWS, 128)
        for zl in range(2):
            for ct in range(4):
                columns = pl.ds((zl * 4 + ct) * 128, 128)
                for row in range(2):
                    for zh in range(4):
                        if i == 0:
                            xs[2 * h, pl.ds(row * 64 + zh * 16, 16), columns] = flat[
                                pl.ds(zh * 256 + zl * 128 + ct * 2 + row, 16, stride=8), :]
                        else:
                            for c in range(2):
                                xs[2 * h + 1, pl.ds(row * 64 + zh * 16 + c * 8, 8), columns] = flat[
                                    pl.ds(zh * 32 + zl * 16 + c * 8 + ct * 2 + row, 8, stride=128), :]

    def give(h, i, new):
        flat = (v1, v2)[i].at[h].reshape(ROWS, 128)
        for zl in range(2):
            for ct in range(4):
                tile = new[:, (zl * 4 + ct) * 128:(zl * 4 + ct + 1) * 128]
                for row in range(2):
                    for zh in range(4):
                        first = row * 64 + zh * 16
                        if i == 0:
                            flat[pl.ds(zh * 256 + zl * 128 + ct * 2 + row, 16, stride=8), :] = tile[first:first + 16]
                        else:
                            for c in range(2):
                                flat[pl.ds(zh * 32 + zl * 16 + c * 8 + ct * 2 + row, 8, stride=128), :] = tile[
                                    first + c * 8:first + c * 8 + 8]

    def renew(u, first, rows):
        at = pl.ds(pl.multiple_of(u * ROWS + first, 8), rows)
        fresh = final[u, pl.ds(first // 8, rows // 8)].reshape(rows, 128)
        out[at, :] = (1.0 - learn_rate * decay_rate) * we[at, :] - learn_rate * fresh

    for u in range(2 * HALVES):
        loads[u][0].wait()
        loads[u][1].wait()
        rows = pl.ds(u * ROWS, ROWS)
        slope = sl[rows, :]
        fresh = hold_rate * mo[rows, :] + slope
        momentum[rows, :] = fresh
        direct[u] = hold_rate * fresh + slope
    pl.semaphore_wait(barrier, (NY - 1) + (NZC - 1) + (NX - 1))
    for h in range(HALVES):
        start(*out1_a(h))
        start(*out1_b(h))
    for h in range(HALVES):
        t1[h, y] = direct[2 * h, pl.ds(pl.multiple_of(y * 128, 128), 128)]
        t2[h, zc] = direct[2 * h + 1, pl.ds(pl.multiple_of(zc * 64, 64), 64)]

    for h in range(HALVES):
        wait_recv(*out1_a(h))
        start(*out2_a(h))
        wait_recv(*out1_b(h))
        start(*out2_b(h))
        r1[h, zc] = t1[h, :, pl.ds(pl.multiple_of(zc * 8, 8), 8)]
        r2[h, y] = t2[h, :, pl.ds(pl.multiple_of(y * 8, 8), 8)]

    row_id = lax.broadcasted_iota(jnp.int32, (128, 128), 0)
    col_id = lax.broadcasted_iota(jnp.int32, (128, 128), 1)
    eye = (row_id == col_id).astype(jnp.float32)
    inner = ((1,), (0,))

    for h in range(HALVES):
        for i, plan in enumerate((out2_a, out2_b)):
            wait_recv(*plan(h))
            take(h, i)
            a = xs[2 * h + i]
            gs[2 * h + i] = dot(a, a, ((1,), (1,)))
            for k in (2, 1, 3):
                x_copy(2 * h + i, lax.rem(x + k, NX)).start()
            gr[2 * h + i, x] = gs[2 * h + i]
        if h > 0:
            wait_recv(*back1_a(h - 1))
            start(*back2_a(h - 1))
            wait_recv(*back1_b(h - 1))
            start(*back2_b(h - 1))
        grams, scales, totals = [], [], []
        for i in range(2):
            at = 2 * h + i
            x_all(at).wait_recv()
            gram = (gr[at, 0] + gr[at, 1]) + (gr[at, 2] + gr[at, 3])
            scale = lax.rsqrt(jnp.sum(jnp.sum(gram * eye, axis=1, keepdims=True), axis=0, keepdims=True) + 1e-06)
            scales.append(scale)
            grams.append(gram * (scale * scale))
        for step in range(3):
            mixes = [3.4445 * eye - 4.775 * g + 2.0315 * dot(g, g, inner) for g in grams]
            if step == 0:
                totals = [s * m for s, m in zip(scales, mixes)]
            if step < 2:
                halves = [dot(m, g, inner) for m, g in zip(mixes, grams)]
                grams = [dot(a, m, inner) for a, m in zip(halves, mixes)]
            if step > 0:
                totals = [dot(m, t, inner) for m, t in zip(mixes, totals)]
        for i, plan in enumerate((back1_a, back1_b)):
            give(h, i, dot(totals[i], xs[2 * h + i], inner))
            start(*plan(h))
            if i == 0:
                w1[h, zc] = v1[h, zc]
            else:
                w2[h, y] = v2[h, y]

    h = HALVES - 1
    for plan in (back1_a, back1_b):
        wait_recv(*plan(h))
        start(*((back2_a, back2_b)[plan is back1_b](h)))
    load_weights.wait()
    for g in range(HALVES):
        final[2 * g, pl.ds(y * 16, 16)] = w1[g, :, y]
        final[2 * g + 1, pl.ds(zc * 8, 8)] = w2[g, :, zc]
        renew(2 * g, y * 128, 128)
        renew(2 * g + 1, zc * 64, 64)
    for g in range(HALVES):
        for plan in (out1_a, out1_b, out2_a, out2_b):
            wait_send(*plan(g))
        for i in range(2):
            x_all(2 * g + i).wait_send()

    for g in range(HALVES):
        for plan in (back1_a, back1_b):
            wait_send(*plan(g))
    for g in range(HALVES):
        wait_recv(*back2_a(g))

        def from_y(k, carry):
            renew(2 * g, lax.rem(y + 1 + k, NY) * 128, 128)
            return carry

        lax.fori_loop(0, NY - 1, from_y, 0)
        wait_recv(*back2_b(g))

        def from_z(k, carry):
            renew(2 * g + 1, lax.rem(zc + 1 + k, NZC) * 64, 64)
            return carry

        lax.fori_loop(0, NZC - 1, from_z, 0)
    for g in range(HALVES):
        for plan in (back2_a, back2_b):
            wait_send(*plan(g))


def body(slopes_in, moments_in, weights_in):
    mats, side, wide = slopes_in.shape

    def flat(a):
        return a.reshape(mats, side, wide // 128, 128).transpose(0, 2, 1, 3).reshape(mats * side * wide // 128, 128)

    def whole(a):
        return a.reshape(mats, wide // 128, side, 128).transpose(0, 2, 1, 3).reshape(mats, side, wide)

    f32 = jnp.float32
    shape = (mats * side * wide // 128, 128)
    vmem = pltpu.VMEM
    dma = pltpu.SemaphoreType.DMA
    out, momentum = pl.pallas_call(
        kernel,
        out_shape=(jax.ShapeDtypeStruct(shape, f32),) * 2,
        in_specs=[pl.BlockSpec(memory_space=pltpu.HBM)] * 3,
        out_specs=[pl.BlockSpec(memory_space=pltpu.VMEM)] * 2,
        scratch_shapes=[
            vmem(shape, f32), vmem(shape, f32), vmem(shape, f32),
            vmem((4, ROWS, 128), f32),
            vmem((HALVES, NY, 128, 128), f32), vmem((HALVES, NZC, 64, 128), f32),
            vmem((HALVES, NZC, NY, 8, 128), f32), vmem((HALVES, NY, NZC, 8, 128), f32),
            vmem((2 * HALVES, 128, 1024), f32),
            vmem((2 * HALVES, 128, 128), f32), vmem((2 * HALVES, NX, 128, 128), f32),
            vmem((HALVES, NZC, NY, 8, 128), f32), vmem((HALVES, NY, NZC, 8, 128), f32),
            vmem((HALVES, NZC, NY, 8, 128), f32), vmem((HALVES, NY, NZC, 8, 128), f32),
            vmem((4, 128, 8, 128), f32),
            dma((2 * HALVES + 1, 2)),
            dma((4 * HALVES,)), dma((4 * HALVES,)), dma((4 * HALVES,)), dma((4 * HALVES,)),
            dma((2 * HALVES,)), dma((2 * HALVES,)),
        ],
        compiler_params=pltpu.CompilerParams(
            collective_id=0, has_side_effects=True, vmem_limit_bytes=48 * 1024 * 1024),
        name="exchange",
    )(flat(slopes_in), flat(moments_in), flat(weights_in))
    return whole(out), whole(momentum)


def solution(mesh):
    spec = P(None, "zero", "width")
    return jax.shard_map(body, mesh=mesh, in_specs=(spec,) * 3, out_specs=(spec,) * 2, check_vma=False)
```

time: 129 us -> 121 us (0.938); the launches traced: 127 us -> 121 us
  Pallas kernels: 124 us -> 118 us
    pallas_call x1, Pallas kernels: 124 us -> 118 us  [body(): pl.pallas_call(kernel, out_shape=(jax.ShapeDtypeStruct(shape, f32),) * 2,...]
where the time goes in v2:
time: 121 us
  Pallas kernels  118 us (98%)
  local copies, waits for them, and re-layouts  2.64 us (2%)
    pallas_call x1, Pallas kernels, body(): pl.pallas_call(kernel, out_shape=(jax.ShapeDtypeStruct(shape, f32),) * 2,...  118 us
    unnamed x2, local copies, waits for them, and re-layouts  2.64 us

profile of v2, /device:TPU:1, one launch (start us, length us, event | category | flops | bytes accessed | tf_op | source)
XLA Modules:
  0.0 120.8 jit_solution(976472198333851533)
XLA Ops:
  0.6 117.6 %exchange.1 = (f32[4096,128]{1,0:T(8,128)S(1)}, f32[4096,128]{1,0:T(8,128)S(1)}) custom-call(f32[4096,128]{1,0:T(8,128)} %bitcast.27, f32[4096,128]{1,0:T(8,128)} %bitcast.28, f32[4096,128]{1,0:T(8,128)} %bitcast.29), custom_call_target="tpu_custom_call" | custom-call | tf_op jit(solution)/shard_map/exchange/pallas_call | solution.py:321
  118.2 1.3 %copy.12 = f32[512,2,512]{2,1,0:T(2,128)} copy(f32[512,2,512]{2,1,0:T(2,128)S(1)} %bitcast.26) | data formatting | bytes 4194304
  119.5 1.3 %copy.13 = f32[512,2,512]{2,1,0:T(2,128)} copy(f32[512,2,512]{2,1,0:T(2,128)S(1)} %bitcast.25) | data formatting | bytes 4194304

commit v3 on v2

v3 whole, which is shorter than its diff:
```python
import jax
import jax.numpy as jnp
from jax import lax
from jax.experimental import pallas as pl
from jax.experimental.pallas import tpu as pltpu
from jax.sharding import PartitionSpec as P

MESH = pl.DeviceIdType.MESH

hold_rate = 0.8
learn_rate = 0.8
decay_rate = 0.1

NX, NY, NZ, NC = 4, 8, 8, 2
NZC = NZ * NC
HALVES = 2
ROWS = 1024


def dot(a, b, contract):
    return lax.dot_general(
        a, b, (contract, ((), ())), precision=lax.Precision.HIGHEST, preferred_element_type=jnp.float32
    )


def ring_step(k, n):
    d = (n - k) // 2
    return d + lax.rem(k, 2) * (n - 2 * d)


def kernel(
    slopes, moments, weights, out, momentum,
    sl, mo, we, direct, t1, t2, r1, r2, xs, gs, gr, v1, v2, w1, w2, final,
    in_sem, send_sem, recv_sem, x_send, x_recv,
):
    zero = lax.axis_index("zero")
    width = lax.axis_index("width")
    core = lax.rem(zero, NC)
    y = lax.rem(zero // NC, NY)
    zh = zero // (NC * NY)
    x = lax.rem(width, NX)
    own = (width // NX) * NC + core
    zc = zh * 4 + own

    def device(px, py, pzh, quarter):
        return ((pzh * NY + py) * NC + lax.rem(quarter, NC), (quarter // NC) * NX + px)

    def y_partner(k, back):
        d = ring_step(k, NY)
        return lax.rem(y + NY - d, NY) if back else lax.rem(y + d, NY)

    def z_partner(g, k, back):
        if g == 0:
            idx, quarter = 0, k
        elif g == 1:
            idx, quarter = 1 + 2 * lax.rem(k, 2), k // 2
        else:
            idx, quarter = 2, lax.rem(own + 1 + k, 4)
        return idx, quarter, lax.rem(zh + (idx + 2 if back else 6 - idx), 4)

    Z_FAR, Z_NEAR = ((0, 4),), ((1, 8), (2, 3))
    Z_ALL = Z_FAR + Z_NEAR
    Y_FAR, Y_NEAR = ((0, 3),), ((3, NY - 1),)
    Y_ALL = ((0, NY - 1),)

    def loop(lo, hi, step):
        def body(k, carry):
            step(k)
            return carry
        lax.fori_loop(lo, hi, body, 0)

    loads = []
    for u in range(2 * HALVES):
        rows = pl.ds(u * ROWS, ROWS)
        loads.append((
            pltpu.make_async_copy(slopes.at[rows], sl.at[rows], in_sem.at[u, 0]),
            pltpu.make_async_copy(moments.at[rows], mo.at[rows], in_sem.at[u, 1]),
        ))
    for a, b in loads:
        a.start()
        b.start()

    barrier = pltpu.get_barrier_semaphore()

    def greet(target):
        pl.semaphore_signal(barrier, inc=1, device_id=target, device_id_type=MESH)

    for g, n in Z_ALL:
        def greet_z(k):
            _, quarter, pzh = z_partner(g, k, False)
            greet(device(x, y, pzh, quarter))
        loop(0, n, greet_z)
    loop(0, NY - 1, lambda k: greet(device(x, y_partner(k, False), zh, own)))
    loop(1, NX, lambda k: greet(device(lax.rem(x + k, NX), y, zh, own)))

    load_weights = pltpu.make_async_copy(weights, we, in_sem.at[2 * HALVES, 0])
    load_weights.start()

    def remote(s, src, dst, target):
        return pltpu.make_async_remote_copy(
            src_ref=src, dst_ref=dst, send_sem=send_sem.at[s], recv_sem=recv_sem.at[s],
            device_id=target, device_id_type=MESH)

    class Along:
        def __init__(self, axis, s, groups, back, src, dst, whole):
            self.axis, self.s, self.groups, self.back = axis, s, groups, back
            self.src, self.dst, self.whole = src, dst, whole

        def copy(self, g, k):
            if self.axis == "y":
                p = y_partner(k, self.back)
                return remote(self.s, self.src(k, p), self.dst(k), device(x, p, zh, own))
            idx, quarter, pzh = z_partner(g, k, self.back)
            return remote(self.s, self.src(idx * 4 + quarter, pzh * 4 + quarter), self.dst(idx * 4 + own),
                          device(x, y, pzh, quarter))

        def start(self):
            for g, n in self.groups:
                if self.axis == "y":
                    loop(g, n, lambda k: self.copy(0, k).start())
                else:
                    loop(0, n, lambda k: self.copy(g, k).start())

        def all(self):
            return remote(self.s, self.whole, self.whole, device(x, lax.rem(y + 1, NY), zh, own))

    def x_copy(s, px):
        return pltpu.make_async_remote_copy(
            src_ref=gs.at[s], dst_ref=gr.at[s, x], send_sem=x_send.at[s], recv_sem=x_recv.at[s],
            device_id=device(px, y, zh, own), device_id_type=MESH)

    def x_all(s):
        whole = gr.at[s, pl.ds(0, NX - 1)]
        return pltpu.make_async_remote_copy(
            src_ref=whole, dst_ref=whole, send_sem=x_send.at[s], recv_sem=x_recv.at[s],
            device_id=device(lax.rem(x + 1, NX), y, zh, own), device_id_type=MESH)

    out1, out2, back1, back2 = [], [], [], []
    for h in range(HALVES):
        a, b = 2 * h, 2 * h + 1
        out1.append((
            Along("y", 12 * h, Y_ALL, False, lambda k, p, a=a: direct.at[a, pl.ds(p * 128, 128)],
                  lambda k, h=h: t1.at[h, k], t1.at[h, pl.ds(0, NY - 1)]),
            Along("z", 12 * h + 1, Z_ALL, False, lambda k, p, b=b: direct.at[b, pl.ds(p * 64, 64)],
                  lambda k, h=h: t2.at[h, k], t2.at[h, pl.ds(0, NZC - 1)]),
        ))
        out2.append((
            Along("z", 12 * h + 2, Z_ALL, False, lambda k, p, h=h: t1.at[h, :, pl.ds(p * 8, 8)],
                  lambda k, h=h: r1.at[h, zc], r1.at[h, pl.ds(0, NZC - 1)]),
            Along("y", 12 * h + 3, Y_ALL, False, lambda k, p, h=h: t2.at[h, :, pl.ds(p * 8, 8)],
                  lambda k, h=h: r2.at[h, y], r2.at[h, pl.ds(0, NY - 1)]),
        ))
        back1.append([])
        back2.append([])
        for part in range(2):
            ya, yb = (pl.ds(0, 3), pl.ds(3, 5))[part], (pl.ds(0, 4), pl.ds(4, 12))[part]
            s = 12 * h + 4 + 4 * part
            back1[h].append((
                Along("z", s, Z_ALL, False, lambda k, p, h=h, ya=ya: v1.at[h, p, ya],
                      lambda k, h=h, ya=ya: w1.at[h, zc, ya], w1.at[h, pl.ds(0, NZC - 1), ya]),
                Along("y", s + 1, Y_ALL, False, lambda k, p, h=h, yb=yb: v2.at[h, p, yb],
                      lambda k, h=h, yb=yb: w2.at[h, y, yb], w2.at[h, pl.ds(0, NY - 1), yb]),
            ))
            back2[h].append((
                Along("y", s + 2, (Y_FAR, Y_NEAR)[part], True, lambda k, p, h=h: w1.at[h, :, k],
                      lambda k, a=a: final.at[a, pl.ds(y * 16, 16)], final.at[a, pl.ds(0, (48, 64)[part])]),
                Along("z", s + 3, (Z_FAR, Z_NEAR)[part], True, lambda k, p, h=h: w2.at[h, :, k],
                      lambda k, b=b: final.at[b, pl.ds(zc * 8, 8)], final.at[b, pl.ds(0, (32, 88)[part])]),
            ))

    def take(h, i):
        flat = (r1, r2)[i].at[h].reshape(ROWS, 128)
        for zl in range(2):
            for ct in range(4):
                columns = pl.ds((zl * 4 + ct) * 128, 128)
                for row in range(2):
                    for zh in range(4):
                        if i == 0:
                            xs[2 * h, pl.ds(row * 64 + zh * 16, 16), columns] = flat[
                                pl.ds(zh * 256 + zl * 128 + ct * 2 + row, 16, stride=8), :]
                        else:
                            for c in range(2):
                                xs[2 * h + 1, pl.ds(row * 64 + zh * 16 + c * 8, 8), columns] = flat[
                                    pl.ds(zh * 32 + zl * 16 + c * 8 + ct * 2 + row, 8, stride=128), :]

    def give(h, i, new):
        flat = (v1, v2)[i].at[h].reshape(ROWS, 128)
        for zl in range(2):
            for ct in range(4):
                tile = new[:, (zl * 4 + ct) * 128:(zl * 4 + ct + 1) * 128]
                for row in range(2):
                    for zh in range(4):
                        first = row * 64 + zh * 16
                        if i == 0:
                            flat[pl.ds(zh * 256 + zl * 128 + ct * 2 + row, 16, stride=8), :] = tile[first:first + 16]
                        else:
                            for c in range(2):
                                flat[pl.ds(zh * 32 + zl * 16 + c * 8 + ct * 2 + row, 8, stride=128), :] = tile[
                                    first + c * 8:first + c * 8 + 8]

    def renew(u, first, rows):
        at = pl.ds(pl.multiple_of(u * ROWS + first, 8), rows)
        fresh = final[u, pl.ds(first // 8, rows // 8)].reshape(rows, 128)
        out[at, :] = (1.0 - learn_rate * decay_rate) * we[at, :] - learn_rate * fresh

    for u in range(2 * HALVES):
        loads[u][0].wait()
        loads[u][1].wait()
        rows = pl.ds(u * ROWS, ROWS)
        slope = sl[rows, :]
        fresh = hold_rate * mo[rows, :] + slope
        momentum[rows, :] = fresh
        direct[u] = hold_rate * fresh + slope
        if u == 0:
            pl.semaphore_wait(barrier, (NY - 1) + (NZC - 1) + (NX - 1))
        out1[u // 2][u % 2].start()
    for h in range(HALVES):
        t1[h, NY - 1] = direct[2 * h, pl.ds(pl.multiple_of(y * 128, 128), 128)]
        t2[h, 8 + own] = direct[2 * h + 1, pl.ds(pl.multiple_of(zc * 64, 64), 64)]

    for h in range(HALVES):
        for i in range(2):
            out1[h][i].all().wait_recv()
            out2[h][i].start()
        r1[h, zc] = t1[h, :, pl.ds(pl.multiple_of(zc * 8, 8), 8)]
        r2[h, y] = t2[h, :, pl.ds(pl.multiple_of(y * 8, 8), 8)]

    row_id = lax.broadcasted_iota(jnp.int32, (128, 128), 0)
    col_id = lax.broadcasted_iota(jnp.int32, (128, 128), 1)
    eye = (row_id == col_id).astype(jnp.float32)
    inner = ((1,), (0,))

    def forward(h):
        for part in range(2):
            for i in range(2):
                back1[h][part][i].all().wait_recv()
                back2[h][part][i].start()

    for h in range(HALVES):
        for i in range(2):
            out2[h][i].all().wait_recv()
            take(h, i)
            a = xs[2 * h + i]
            gs[2 * h + i] = dot(a, a, ((1,), (1,)))
            for k in (2, 1, 3):
                x_copy(2 * h + i, lax.rem(x + k, NX)).start()
            gr[2 * h + i, x] = gs[2 * h + i]
        if h > 0:
            forward(h - 1)
        grams, scales, totals = [], [], []
        for i in range(2):
            at = 2 * h + i
            x_all(at).wait_recv()
            gram = (gr[at, 0] + gr[at, 1]) + (gr[at, 2] + gr[at, 3])
            scale = lax.rsqrt(jnp.sum(jnp.sum(gram * eye, axis=1, keepdims=True), axis=0, keepdims=True) + 1e-06)
            scales.append(scale)
            grams.append(gram * (scale * scale))
        for step in range(3):
            mixes = [3.4445 * eye - 4.775 * g + 2.0315 * dot(g, g, inner) for g in grams]
            if step == 0:
                totals = [s * m for s, m in zip(scales, mixes)]
            if step < 2:
                halves = [dot(m, g, inner) for m, g in zip(mixes, grams)]
                grams = [dot(a, m, inner) for a, m in zip(halves, mixes)]
            if step > 0:
                totals = [dot(m, t, inner) for m, t in zip(mixes, totals)]
        for i in range(2):
            give(h, i, dot(totals[i], xs[2 * h + i], inner))
            for part in range(2):
                back1[h][part][i].start()
            if i == 0:
                w1[h, zc] = v1[h, zc]
            else:
                w2[h, y] = v2[h, y]

    forward(HALVES - 1)
    load_weights.wait()
    for g in range(HALVES):
        final[2 * g, pl.ds(y * 16, 16)] = w1[g, :, NY - 1]
        final[2 * g + 1, pl.ds(zc * 8, 8)] = w2[g, :, 8 + own]
        renew(2 * g, y * 128, 128)
    for g in range(HALVES):
        for pair in (out1[g], out2[g], back1[g][0], back1[g][1]):
            for one in pair:
                one.all().wait_send()
        for i in range(2):
            x_all(2 * g + i).wait_send()
    for g in range(HALVES):
        for part in range(2):
            back2[g][part][0].all().wait_recv()
            for lo, hi in (Y_FAR, Y_NEAR)[part]:
                loop(lo, hi, lambda k: renew(2 * g, y_partner(k, False) * 128, 128))
            back2[g][part][1].all().wait_recv()
            for idx in ((0,), (1, 3, 2))[part]:
                renew(2 * g + 1, lax.rem(zh + 6 - idx, 4) * 256, 256)
    for g in range(HALVES):
        for pair in back2[g]:
            for one in pair:
                one.all().wait_send()


PIECES = 4


def land(out, momentum, out_hbm, momentum_hbm, sem):
    copies = []
    for i in range(PIECES):
        rows = pl.ds(i * (out.shape[0] // PIECES), out.shape[0] // PIECES)
        copies.append(pltpu.make_async_copy(out.at[rows], out_hbm.at[rows], sem.at[0, i]))
        copies.append(pltpu.make_async_copy(momentum.at[rows], momentum_hbm.at[rows], sem.at[1, i]))
    for copy in copies:
        copy.start()
    for copy in copies:
        copy.wait()


def body(slopes_in, moments_in, weights_in):
    mats, side, wide = slopes_in.shape

    def flat(a):
        return a.reshape(mats, side, wide // 128, 128).transpose(0, 2, 1, 3).reshape(mats * side * wide // 128, 128)

    def whole(a):
        return a.reshape(mats, wide // 128, side, 128).transpose(0, 2, 1, 3).reshape(mats, side, wide)

    f32 = jnp.float32
    shape = (mats * side * wide // 128, 128)
    vmem = pltpu.VMEM
    dma = pltpu.SemaphoreType.DMA
    out, momentum = pl.pallas_call(
        kernel,
        out_shape=(jax.ShapeDtypeStruct(shape, f32),) * 2,
        in_specs=[pl.BlockSpec(memory_space=pltpu.HBM)] * 3,
        out_specs=[pl.BlockSpec(memory_space=pltpu.VMEM)] * 2,
        scratch_shapes=[
            vmem(shape, f32), vmem(shape, f32), vmem(shape, f32),
            vmem((4, ROWS, 128), f32),
            vmem((HALVES, NY, 128, 128), f32), vmem((HALVES, NZC, 64, 128), f32),
            vmem((HALVES, NZC, NY, 8, 128), f32), vmem((HALVES, NY, NZC, 8, 128), f32),
            vmem((2 * HALVES, 128, 1024), f32),
            vmem((2 * HALVES, 128, 128), f32), vmem((2 * HALVES, NX, 128, 128), f32),
            vmem((HALVES, NZC, NY, 8, 128), f32), vmem((HALVES, NY, NZC, 8, 128), f32),
            vmem((HALVES, NZC, NY, 8, 128), f32), vmem((HALVES, NY, NZC, 8, 128), f32),
            vmem((4, 128, 8, 128), f32),
            dma((2 * HALVES + 1, 2)),
            dma((12 * HALVES,)), dma((12 * HALVES,)),
            dma((2 * HALVES,)), dma((2 * HALVES,)),
        ],
        compiler_params=pltpu.CompilerParams(
            collective_id=0, has_side_effects=True, vmem_limit_bytes=48 * 1024 * 1024),
        name="exchange",
    )(flat(slopes_in), flat(moments_in), flat(weights_in))
    out, momentum = pl.pallas_call(
        land,
        out_shape=(jax.ShapeDtypeStruct(shape, f32),) * 2,
        in_specs=[pl.BlockSpec(memory_space=pltpu.VMEM)] * 2,
        out_specs=[pl.BlockSpec(memory_space=pltpu.HBM)] * 2,
        scratch_shapes=[dma((2, PIECES))],
        compiler_params=pltpu.CompilerParams(vmem_limit_bytes=16 * 1024 * 1024),
        name="land",
    )(out, momentum)
    return whole(out), whole(momentum)


def solution(mesh):
    spec = P(None, "zero", "width")
    return jax.shard_map(body, mesh=mesh, in_specs=(spec,) * 3, out_specs=(spec,) * 2, check_vma=False)
```

time: 121 us -> 118 us (0.975)
  local copies, waits for them, and re-layouts: 2.64 us -> 0 us
    unnamed x2 -> x0, local copies, waits for them, and re-layouts: 2.64 us -> none
    pallas_call x1, Pallas kernels: 118 us -> 115 us  [body(): pl.pallas_call(kernel, out_shape=(jax.ShapeDtypeStruct(shape, f32),) * 2,...]
    pallas_call x0 -> x1, Pallas kernels: none -> 2.07 us  [body(): pl.pallas_call(land, out_shape=(jax.ShapeDtypeStruct(shape, f32),) * 2, i...]
where the time goes in v3:
time: 118 us
  Pallas kernels  117 us (99%)
    pallas_call x1, Pallas kernels, body(): pl.pallas_call(kernel, out_shape=(jax.ShapeDtypeStruct(shape, f32),) * 2,...  115 us

profile of v3, /device:TPU:1, one launch (start us, length us, event | category | flops | bytes accessed | tf_op | source)
XLA Modules:
  0.0 117.8 jit_solution(13469984325735021620)
XLA Ops:
  0.6 115.1 %exchange.1 = (f32[4096,128]{1,0:T(8,128)S(1)}, f32[4096,128]{1,0:T(8,128)S(1)}) custom-call(f32[4096,128]{1,0:T(8,128)} %bitcast.25, f32[4096,128]{1,0:T(8,128)} %bitcast.26, f32[4096,128]{1,0:T(8,128)} %bitcast.27), custom_call_target="tpu_custom_call" | custom-call | tf_op jit(solution)/shard_map/exchange/pallas_call | solution.py:330
  115.7 2.1 %land.1 = (f32[4096,128]{1,0:T(8,128)}, f32[4096,128]{1,0:T(8,128)}) custom-call(f32[4096,128]{1,0:T(8,128)S(1)} %get-tuple-element.6.out, f32[4096,128]{1,0:T(8,128)S(1)} %get-tuple-element.7.momentum), custom_call_target="tpu_custom_call" | custom-call | tf_op jit(solution)/shard_map/land/pallas_call | solution.py:353

commit v4 on v3

--- a/solution.py
+++ b/solution.py
@@ -24,7 +24,7 @@
 
 
 def ring_step(k, n):
-    d = (n - k) // 2
+    d = lax.div(n - k, 2)
     return d + lax.rem(k, 2) * (n - 2 * d)
 
 
@@ -36,14 +36,14 @@
     zero = lax.axis_index("zero")
     width = lax.axis_index("width")
     core = lax.rem(zero, NC)
-    y = lax.rem(zero // NC, NY)
-    zh = zero // (NC * NY)
+    y = lax.rem(lax.div(zero, NC), NY)
+    zh = lax.div(zero, NC * NY)
     x = lax.rem(width, NX)
-    own = (width // NX) * NC + core
+    own = lax.div(width, NX) * NC + core
     zc = zh * 4 + own
 
     def device(px, py, pzh, quarter):
-        return ((pzh * NY + py) * NC + lax.rem(quarter, NC), (quarter // NC) * NX + px)
+        return ((pzh * NY + py) * NC + lax.rem(quarter, NC), lax.div(quarter, NC) * NX + px)
 
     def y_partner(k, back):
         d = ring_step(k, NY)
@@ -53,7 +53,7 @@
         if g == 0:
             idx, quarter = 0, k
         elif g == 1:
-            idx, quarter = 1 + 2 * lax.rem(k, 2), k // 2
+            idx, quarter = 1 + 2 * lax.rem(k, 2), lax.div(k, 2)
         else:
             idx, quarter = 2, lax.rem(own + 1 + k, 4)
         return idx, quarter, lax.rem(zh + (idx + 2 if back else 6 - idx), 4)
@@ -68,6 +68,23 @@
             step(k)
             return carry
         lax.fori_loop(lo, hi, body, 0)
+
+    barrier = pltpu.get_barrier_semaphore()
+
+    def greet(target):
+        pl.semaphore_signal(barrier, inc=1, device_id=target, device_id_type=MESH)
+
+    for d in (2, 1, 3, 0):
+        pzh = lax.rem(zh + d, 4)
+        for q in range(4):
+            if d > 0:
+                greet(device(x, y, pzh, q))
+            elif q > 0:
+                greet(device(x, y, pzh, lax.rem(own + q, 4)))
+    for d in (4, 3, 5, 2, 6, 1, 7):
+        greet(device(x, lax.rem(y + d, NY), zh, own))
+    for d in (2, 1, 3):
+        greet(device(lax.rem(x + d, NX), y, zh, own))
 
     loads = []
     for u in range(2 * HALVES):
@@ -79,19 +96,6 @@
     for a, b in loads:
         a.start()
         b.start()
-
-    barrier = pltpu.get_barrier_semaphore()
-
-    def greet(target):
-        pl.semaphore_signal(barrier, inc=1, device_id=target, device_id_type=MESH)
-
-    for g, n in Z_ALL:
-        def greet_z(k):
-            _, quarter, pzh = z_partner(g, k, False)
-            greet(device(x, y, pzh, quarter))
-        loop(0, n, greet_z)
-    loop(0, NY - 1, lambda k: greet(device(x, y_partner(k, False), zh, own)))
-    loop(1, NX, lambda k: greet(device(lax.rem(x + k, NX), y, zh, own)))
 
     load_weights = pltpu.make_async_copy(weights, we, in_sem.at[2 * HALVES, 0])
     load_weights.start()
@@ -230,6 +234,19 @@
     eye = (row_id == col_id).astype(jnp.float32)
     inner = ((1,), (0,))
 
+    low_lanes = col_id[:32] < 64
+
+    def pack(gram):
+        corner = jnp.where(low_lanes, pltpu.roll(gram[64:96], 64, 1), gram[96:])
+        return jnp.concatenate([gram[:64], corner], axis=0)
+
+    def unpack(packed):
+        corner = packed[64:]
+        corner = jnp.concatenate([pltpu.roll(corner, 64, 1), corner], axis=0)
+        mirrored = jnp.concatenate([packed[:64], jnp.zeros((64, 128), jnp.float32)], axis=0).T
+        lower = jnp.where(col_id[:64] < 64, mirrored[64:], corner)
+        return jnp.concatenate([packed[:64], lower], axis=0)
+
     def forward(h):
         for part in range(2):
             for i in range(2):
@@ -241,7 +258,7 @@
             out2[h][i].all().wait_recv()
             take(h, i)
             a = xs[2 * h + i]
-            gs[2 * h + i] = dot(a, a, ((1,), (1,)))
+            gs[2 * h + i] = pack(dot(a, a, ((1,), (1,))))
             for k in (2, 1, 3):
                 x_copy(2 * h + i, lax.rem(x + k, NX)).start()
             gr[2 * h + i, x] = gs[2 * h + i]
@@ -251,7 +268,7 @@
         for i in range(2):
             at = 2 * h + i
             x_all(at).wait_recv()
-            gram = (gr[at, 0] + gr[at, 1]) + (gr[at, 2] + gr[at, 3])
+            gram = unpack((gr[at, 0] + gr[at, 1]) + (gr[at, 2] + gr[at, 3]))
             scale = lax.rsqrt(jnp.sum(jnp.sum(gram * eye, axis=1, keepdims=True), axis=0, keepdims=True) + 1e-06)
             scales.append(scale)
             grams.append(gram * (scale * scale))
@@ -266,12 +283,13 @@
                 totals = [dot(m, t, inner) for m, t in zip(mixes, totals)]
         for i in range(2):
             give(h, i, dot(totals[i], xs[2 * h + i], inner))
-            for part in range(2):
-                back1[h][part][i].start()
+            back1[h][0][i].start()
             if i == 0:
                 w1[h, zc] = v1[h, zc]
             else:
                 w2[h, y] = v2[h, y]
+        for i in range(2):
+            back1[h][1][i].start()
 
     forward(HALVES - 1)
     load_weights.wait()
@@ -338,7 +356,7 @@
             vmem((HALVES, NY, 128, 128), f32), vmem((HALVES, NZC, 64, 128), f32),
             vmem((HALVES, NZC, NY, 8, 128), f32), vmem((HALVES, NY, NZC, 8, 128), f32),
             vmem((2 * HALVES, 128, 1024), f32),
-            vmem((2 * HALVES, 128, 128), f32), vmem((2 * HALVES, NX, 128, 128), f32),
+            vmem((2 * HALVES, 96, 128), f32), vmem((2 * HALVES, NX, 96, 128), f32),
             vmem((HALVES, NZC, NY, 8, 128), f32), vmem((HALVES, NY, NZC, 8, 128), f32),
             vmem((HALVES, NZC, NY, 8, 128), f32), vmem((HALVES, NY, NZC, 8, 128), f32),
             vmem((4, 128, 8, 128), f32),

time: 118 us -> 116 us (0.983)
  Pallas kernels: 117 us -> 115 us
    pallas_call x1, Pallas kernels: 115 us -> 113 us  [body(): pl.pallas_call(kernel, out_shape=(jax.ShapeDtypeStruct(shape, f32),) * 2,...]
where the time goes in v4:
time: 116 us
  Pallas kernels  115 us (99%)
    pallas_call x1, Pallas kernels, body(): pl.pallas_call(kernel, out_shape=(jax.ShapeDtypeStruct(shape, f32),) * 2,...  113 us

profile of v4, /device:TPU:1, one launch (start us, length us, event | category | flops | bytes accessed | tf_op | source)
XLA Modules:
  0.0 115.8 jit_solution(11991689198048834963)
XLA Ops:
  0.6 113.1 %exchange.1 = (f32[4096,128]{1,0:T(8,128)S(1)}, f32[4096,128]{1,0:T(8,128)S(1)}) custom-call(f32[4096,128]{1,0:T(8,128)} %bitcast.25, f32[4096,128]{1,0:T(8,128)} %bitcast.26, f32[4096,128]{1,0:T(8,128)} %bitcast.27), custom_call_target="tpu_custom_call" | custom-call | tf_op jit(solution)/shard_map/exchange/pallas_call | solution.py:348
  113.7 2.1 %land.1 = (f32[4096,128]{1,0:T(8,128)}, f32[4096,128]{1,0:T(8,128)}) custom-call(f32[4096,128]{1,0:T(8,128)S(1)} %get-tuple-element.6.out, f32[4096,128]{1,0:T(8,128)S(1)} %get-tuple-element.7.momentum), custom_call_target="tpu_custom_call" | custom-call | tf_op jit(solution)/shard_map/land/pallas_call | solution.py:371

commit v5 on v4

--- a/solution.py
+++ b/solution.py
@@ -69,6 +69,17 @@
             return carry
         lax.fori_loop(lo, hi, body, 0)
 
+    loads = []
+    for u in range(2 * HALVES):
+        rows = pl.ds(u * ROWS, ROWS)
+        loads.append((
+            pltpu.make_async_copy(slopes.at[rows], sl.at[rows], in_sem.at[u, 0]),
+            pltpu.make_async_copy(moments.at[rows], mo.at[rows], in_sem.at[u, 1]),
+        ))
+    for a, b in loads:
+        a.start()
+        b.start()
+
     barrier = pltpu.get_barrier_semaphore()
 
     def greet(target):
@@ -86,17 +97,6 @@
     for d in (2, 1, 3):
         greet(device(lax.rem(x + d, NX), y, zh, own))
 
-    loads = []
-    for u in range(2 * HALVES):
-        rows = pl.ds(u * ROWS, ROWS)
-        loads.append((
-            pltpu.make_async_copy(slopes.at[rows], sl.at[rows], in_sem.at[u, 0]),
-            pltpu.make_async_copy(moments.at[rows], mo.at[rows], in_sem.at[u, 1]),
-        ))
-    for a, b in loads:
-        a.start()
-        b.start()
-
     load_weights = pltpu.make_async_copy(weights, we, in_sem.at[2 * HALVES, 0])
     load_weights.start()
 
@@ -106,9 +106,9 @@
             device_id=target, device_id_type=MESH)
 
     class Along:
-        def __init__(self, axis, s, groups, back, src, dst, whole):
+        def __init__(self, axis, s, groups, back, src, dst, whole, near_first=False):
             self.axis, self.s, self.groups, self.back = axis, s, groups, back
-            self.src, self.dst, self.whole = src, dst, whole
+            self.src, self.dst, self.whole, self.near_first = src, dst, whole, near_first
 
         def copy(self, g, k):
             if self.axis == "y":
@@ -119,11 +119,9 @@
                           device(x, y, pzh, quarter))
 
         def start(self):
-            for g, n in self.groups:
-                if self.axis == "y":
-                    loop(g, n, lambda k: self.copy(0, k).start())
-                else:
-                    loop(0, n, lambda k: self.copy(g, k).start())
+            for g, n in self.groups[::-1] if self.near_first else self.groups:
+                lo = g if self.axis == "y" else 0
+                loop(lo, n, lambda k: self.copy(g, lo + n - 1 - k if self.near_first else k).start())
 
         def all(self):
             return remote(self.s, self.whole, self.whole, device(x, lax.rem(y + 1, NY), zh, own))
@@ -150,9 +148,9 @@
         ))
         out2.append((
             Along("z", 12 * h + 2, Z_ALL, False, lambda k, p, h=h: t1.at[h, :, pl.ds(p * 8, 8)],
-                  lambda k, h=h: r1.at[h, zc], r1.at[h, pl.ds(0, NZC - 1)]),
+                  lambda k, h=h: r1.at[h, zc], r1.at[h, pl.ds(0, NZC - 1)], near_first=True),
             Along("y", 12 * h + 3, Y_ALL, False, lambda k, p, h=h: t2.at[h, :, pl.ds(p * 8, 8)],
-                  lambda k, h=h: r2.at[h, y], r2.at[h, pl.ds(0, NY - 1)]),
+                  lambda k, h=h: r2.at[h, y], r2.at[h, pl.ds(0, NY - 1)], near_first=True),
         ))
         back1.append([])
         back2.append([])
@@ -248,10 +246,9 @@
         return jnp.concatenate([packed[:64], lower], axis=0)
 
     def forward(h):
-        for part in range(2):
-            for i in range(2):
-                back1[h][part][i].all().wait_recv()
-                back2[h][part][i].start()
+        for part, i in ((0, 1), (0, 0), (1, 0), (1, 1)):
+            back1[h][part][i].all().wait_recv()
+            back2[h][part][i].start()
 
     for h in range(HALVES):
         for i in range(2):

time: 116 us -> 114 us (0.983)
  Pallas kernels: 115 us -> 113 us
    pallas_call x1, Pallas kernels: 113 us -> 111 us  [body(): pl.pallas_call(kernel, out_shape=(jax.ShapeDtypeStruct(shape, f32),) * 2,...]
where the time goes in v5:
time: 114 us
  Pallas kernels  113 us (99%)
    pallas_call x1, Pallas kernels, body(): pl.pallas_call(kernel, out_shape=(jax.ShapeDtypeStruct(shape, f32),) * 2,...  111 us

profile of v5, /device:TPU:1, one launch (start us, length us, event | category | flops | bytes accessed | tf_op | source)
XLA Modules:
  0.0 114.0 jit_solution(12825588533040621495)
XLA Ops:
  0.6 111.3 %exchange.1 = (f32[4096,128]{1,0:T(8,128)S(1)}, f32[4096,128]{1,0:T(8,128)S(1)}) custom-call(f32[4096,128]{1,0:T(8,128)} %bitcast.25, f32[4096,128]{1,0:T(8,128)} %bitcast.26, f32[4096,128]{1,0:T(8,128)} %bitcast.27), custom_call_target="tpu_custom_call" | custom-call | tf_op jit(solution)/shard_map/exchange/pallas_call | solution.py:345
  111.9 2.1 %land.1 = (f32[4096,128]{1,0:T(8,128)}, f32[4096,128]{1,0:T(8,128)}) custom-call(f32[4096,128]{1,0:T(8,128)S(1)} %get-tuple-element.6.out, f32[4096,128]{1,0:T(8,128)S(1)} %get-tuple-element.7.momentum), custom_call_target="tpu_custom_call" | custom-call | tf_op jit(solution)/shard_map/land/pallas_call | solution.py:368

commit v6 on v5

--- a/solution.py
+++ b/solution.py
@@ -76,9 +76,8 @@
             pltpu.make_async_copy(slopes.at[rows], sl.at[rows], in_sem.at[u, 0]),
             pltpu.make_async_copy(moments.at[rows], mo.at[rows], in_sem.at[u, 1]),
         ))
-    for a, b in loads:
-        a.start()
-        b.start()
+    for copy in loads[0]:
+        copy.start()
 
     barrier = pltpu.get_barrier_semaphore()
 
@@ -97,8 +96,10 @@
     for d in (2, 1, 3):
         greet(device(lax.rem(x + d, NX), y, zh, own))
 
+    for pair in loads[1:]:
+        for copy in pair:
+            copy.start()
     load_weights = pltpu.make_async_copy(weights, we, in_sem.at[2 * HALVES, 0])
-    load_weights.start()
 
     def remote(s, src, dst, target):
         return pltpu.make_async_remote_copy(
@@ -216,6 +217,7 @@
         if u == 0:
             pl.semaphore_wait(barrier, (NY - 1) + (NZC - 1) + (NX - 1))
         out1[u // 2][u % 2].start()
+    load_weights.start()
     for h in range(HALVES):
         t1[h, NY - 1] = direct[2 * h, pl.ds(pl.multiple_of(y * 128, 128), 128)]
         t2[h, 8 + own] = direct[2 * h + 1, pl.ds(pl.multiple_of(zc * 64, 64), 64)]
@@ -278,8 +280,9 @@
                 grams = [dot(a, m, inner) for a, m in zip(halves, mixes)]
             if step > 0:
                 totals = [dot(m, t, inner) for m, t in zip(mixes, totals)]
-        for i in range(2):
-            give(h, i, dot(totals[i], xs[2 * h + i], inner))
+        news = [dot(totals[i], xs[2 * h + i], inner) for i in range(2)]
+        for i in range(2):
+            give(h, i, news[i])
             back1[h][0][i].start()
             if i == 0:
                 w1[h, zc] = v1[h, zc]

time: 114 us -> 115 us (level)
  no operation moved by 1% of the time
where the time goes in v6:
time: 115 us; the launch traced here: 114 us
  Pallas kernels  114 us (99%)
    pallas_call x1, Pallas kernels, body(): pl.pallas_call(kernel, out_shape=(jax.ShapeDtypeStruct(shape, f32),) * 2,...  112 us

profile of v6, /device:TPU:1, one launch (start us, length us, event | category | flops | bytes accessed | tf_op | source)
XLA Modules:
  0.0 114.5 jit_solution(4442472885749470014)
XLA Ops:
  0.6 111.8 %exchange.1 = (f32[4096,128]{1,0:T(8,128)S(1)}, f32[4096,128]{1,0:T(8,128)S(1)}) custom-call(f32[4096,128]{1,0:T(8,128)} %bitcast.25, f32[4096,128]{1,0:T(8,128)} %bitcast.26, f32[4096,128]{1,0:T(8,128)} %bitcast.27), custom_call_target="tpu_custom_call" | custom-call | tf_op jit(solution)/shard_map/exchange/pallas_call | solution.py:348
  112.4 2.1 %land.1 = (f32[4096,128]{1,0:T(8,128)}, f32[4096,128]{1,0:T(8,128)}) custom-call(f32[4096,128]{1,0:T(8,128)S(1)} %get-tuple-element.6.out, f32[4096,128]{1,0:T(8,128)S(1)} %get-tuple-element.7.momentum), custom_call_target="tpu_custom_call" | custom-call | tf_op jit(solution)/shard_map/land/pallas_call | solution.py:371

commit v7 on v5

--- a/solution.py
+++ b/solution.py
@@ -276,10 +276,11 @@
             if step < 2:
                 halves = [dot(m, g, inner) for m, g in zip(mixes, grams)]
                 grams = [dot(a, m, inner) for a, m in zip(halves, mixes)]
-            if step > 0:
+            if step == 1:
                 totals = [dot(m, t, inner) for m, t in zip(mixes, totals)]
-        for i in range(2):
-            give(h, i, dot(totals[i], xs[2 * h + i], inner))
+                partly = [dot(t, xs[2 * h + i], inner) for i, t in enumerate(totals)]
+        for i in range(2):
+            give(h, i, dot(mixes[i], partly[i], inner))
             back1[h][0][i].start()
             if i == 0:
                 w1[h, zc] = v1[h, zc]

time: 114 us -> 115 us (level)
  no operation moved by 1% of the time
where the time goes in v7:
time: 115 us
  Pallas kernels  114 us (99%)
    pallas_call x1, Pallas kernels, body(): pl.pallas_call(kernel, out_shape=(jax.ShapeDtypeStruct(shape, f32),) * 2,...  112 us

profile of v7, /device:TPU:1, one launch (start us, length us, event | category | flops | bytes accessed | tf_op | source)
XLA Modules:
  0.0 114.7 jit_solution(4466431829140982335)
XLA Ops:
  0.6 112.0 %exchange.1 = (f32[4096,128]{1,0:T(8,128)S(1)}, f32[4096,128]{1,0:T(8,128)S(1)}) custom-call(f32[4096,128]{1,0:T(8,128)} %bitcast.25, f32[4096,128]{1,0:T(8,128)} %bitcast.26, f32[4096,128]{1,0:T(8,128)} %bitcast.27), custom_call_target="tpu_custom_call" | custom-call | tf_op jit(solution)/shard_map/exchange/pallas_call | solution.py:346
  112.6 2.1 %land.1 = (f32[4096,128]{1,0:T(8,128)}, f32[4096,128]{1,0:T(8,128)}) custom-call(f32[4096,128]{1,0:T(8,128)S(1)} %get-tuple-element.6.out, f32[4096,128]{1,0:T(8,128)S(1)} %get-tuple-element.7.momentum), custom_call_target="tpu_custom_call" | custom-call | tf_op jit(solution)/shard_map/land/pallas_call | solution.py:369
